TPU v7x, 32 devices: a whole 2x2x4 slice. The times are simulated.
32 devices in a mesh: job: 2 (over y), row: 4 (over z), col: 2 (over x), samp: 2 (over core).
Axes of the slice: x: 2, y: 2, z: 4, core: 2. Of those that a mesh axis runs over, the one named last changes fastest.
Arguments:
- pair_repr: bfloat16 [256, 128, 128], P(('job', 'row'), ('col', 'samp')), parts along dimension 0, may hold values from -100 to 100
- asym_id: int32 [256], P('job'), parts along dimension 0, may hold values from 0 to 7, never falling along the last dimension, each value on 1 to 32 neighbouring positions
- valid_len: int32 [2], P('job'), parts along dimension 0, may hold values from 64 to 128
- rel_embed: bfloat16 [128, 128], replicated, may hold values from -12 to 12
- pair_gain: float32 [128], replicated, may hold values from 0.25 to 1.75
- bias_weight: bfloat16 [128, 16], replicated, may hold values from -64 to 64
- tokens: bfloat16 [32, 128, 768], P(('job', 'col', 'samp'), 'row'), parts along dimension 0, may hold values from -6 to 6
- token_gain: float32 [1, 768], replicated, may hold values from 0.25 to 1.75
- qkv_weight: bfloat16 [1, 3, 768, 768], P(None, None, None, 'row'), may hold values from -0.21875 to 0.21875
- out_weight: bfloat16 [1, 768, 768], P(None, 'row'), may hold values from -0.21875 to 0.21875
Outputs:
- refined: bfloat16 [32, 128, 768], P(('job', 'col', 'samp'), 'row'), parts along dimension 0
There are 2 independent parts, one for each index of `job`. A program takes and returns all parts, laid end to end along the dimension named above; an argument that names none is the same for every part. Nothing has to cross between parts.
Inputs may be any that keep to these rules, and one draw needn't show every extreme that they name: `asym_id`: chain indices never fall along the tokens.
All inputs are finite; a program needn't handle non-finite values.
Results may differ from a plain program's by a relative error of at most 0.002.
The roundings to bfloat16 on the way count: a program that leaves them out, or rounds other values in their place, can miss the bound.
Values may be sent and summed in bfloat16 or wider, within the bound.
A program may use at most 64 MiB of HBM per device.

v0:
```python
import math
import jax
import jax.numpy as jnp
from jax import lax
from jax.sharding import PartitionSpec as P

HEAD_DIM = 48
epsilon = 1e-05


def normalize(values, gain_vector):
    average = jnp.mean(values, axis=-1, keepdims=True)
    centered = values - average
    variance = jnp.mean(centered * centered, axis=-1, keepdims=True)
    return centered * lax.rsqrt(variance + epsilon) * gain_vector


def bias_tile_of(pair_repr, asym_id, rel_embed, pair_gain, bias_weight):
    tile_rows, tile_cols, channels = pair_repr.shape
    bin_count = rel_embed.shape[0]
    reach_max = bin_count // 2 - 1
    first_row = lax.axis_index("row") * tile_rows
    first_col = lax.axis_index(("col", "samp")) * tile_cols
    row_ids = first_row + jnp.arange(tile_rows, dtype=jnp.int32)
    col_ids = first_col + jnp.arange(tile_cols, dtype=jnp.int32)
    row_chain = lax.dynamic_slice_in_dim(asym_id, first_row, tile_rows, 0)
    col_chain = lax.dynamic_slice_in_dim(asym_id, first_col, tile_cols, 0)
    offset = jnp.clip(row_ids[:, None] - col_ids[None, :], -reach_max, reach_max) + reach_max
    bin_ids = jnp.where(row_chain[:, None] == col_chain[None, :], offset, bin_count - 1)
    onehot = (
        bin_ids.reshape(-1)[:, None] == jnp.arange(bin_count, dtype=jnp.int32)[None, :]
    ).astype(jnp.bfloat16)
    summed = pair_repr.reshape(-1, channels).astype(jnp.float32) + jnp.dot(
        onehot, rel_embed, preferred_element_type=jnp.float32
    )
    normed = normalize(summed, pair_gain).astype(jnp.bfloat16)
    projected = lax.dot_general(
        bias_weight, normed, (((0,), (1,)), ((), ())), preferred_element_type=jnp.float32
    )
    return projected.reshape(bias_weight.shape[1], tile_rows, tile_cols)


def attend(queries, key_rows, value_rows, pair_bias, keymask, score_scale):
    head_count, query_count, key_count = pair_bias.shape
    model_width = queries.shape[-1]
    head_width = model_width // head_count
    query_h = queries.reshape(query_count, head_count, head_width)
    key_h = key_rows.reshape(key_count, head_count, head_width)
    value_h = value_rows.reshape(key_count, head_count, head_width)
    scores = (
        jnp.einsum("ihd,jhd->hij", query_h, key_h, preferred_element_type=jnp.float32) * score_scale
        + pair_bias
    )
    scores = jnp.where(keymask[None, None, :], scores, -1e30)
    row_max = jnp.max(scores, axis=-1, keepdims=True)
    weights = jnp.where(keymask[None, None, :], jnp.exp(scores - row_max), 0.0)
    row_total = jnp.sum(weights, axis=-1, keepdims=True)
    probs = (weights / row_total).astype(jnp.bfloat16)
    attended = jnp.einsum("hij,jhd->ihd", probs, value_h, preferred_element_type=jnp.float32)
    return attended.reshape(query_count, model_width).astype(jnp.bfloat16)


def per_device(
    pair_repr,
    asym_id,
    valid_len,
    rel_embed,
    pair_gain,
    bias_weight,
    tokens,
    token_gain,
    qkv_weight,
    out_weight,
):
    sample_count, token_rows, model_width = tokens.shape
    total_tokens = asym_id.shape[0]
    keymask = jnp.arange(total_tokens, dtype=jnp.int32) < valid_len[0]
    score_scale = 1.0 / math.sqrt(HEAD_DIM)
    bias_tile = bias_tile_of(pair_repr, asym_id, rel_embed, pair_gain, bias_weight)
    head_tile = lax.all_to_all(bias_tile, "row", split_axis=0, concat_axis=1, tiled=True)
    pair_bias = lax.all_gather(head_tile, ("col", "samp"), axis=2, tiled=True)

    def one_sample(sample_item):
        return attend(
            sample_item[0], sample_item[1], sample_item[2], pair_bias, keymask, score_scale
        )

    current = tokens
    normed = normalize(current.astype(jnp.float32), token_gain[0]).astype(jnp.bfloat16)
    layer_weight = qkv_weight[0]
    projected = jnp.einsum(
        "snc,pcw->psnw",
        lax.all_gather(normed, "row", axis=1, tiled=True),
        layer_weight,
        preferred_element_type=jnp.float32,
    ).astype(jnp.bfloat16)
    head_out = lax.map(one_sample, (projected[0], projected[1], projected[2]))
    attended = lax.all_to_all(head_out, "row", split_axis=1, concat_axis=2, tiled=True)
    flattened = attended.reshape(sample_count * token_rows, model_width)
    update = jnp.dot(
        flattened,
        lax.all_gather(out_weight[0], "row", axis=0, tiled=True),
        preferred_element_type=jnp.float32,
    )
    current = (
        current.astype(jnp.float32) + update.reshape(sample_count, token_rows, model_width)
    ).astype(jnp.bfloat16)
    return current


def solution(mesh):
    return jax.shard_map(
        per_device,
        mesh=mesh,
        in_specs=(
            P(("job", "row"), ("col", "samp"), None),
            P("job"),
            P("job"),
            P(),
            P(),
            P(),
            P(("job", "col", "samp"), "row", None),
            P(),
            P(None, None, None, "row"),
            P(None, "row", None),
        ),
        out_specs=P(("job", "col", "samp"), "row", None),
        check_vma=False,
    )
```

profile of v0, /device:TPU:0, one launch (start us, length us, event | category | flops | bytes accessed | tf_op | source)
XLA Modules:
  0.0 80.8 jit_solution(11071996184877069261)
XLA Ops:
  6.5 0.0 copy-start
  6.5 0.0 copy-start.2
  6.5 0.8 %fusion.27 = (s32[32]{0:T(128)S(1)}, s32[32]{0:T(128)S(1)}) fusion(s32[128]{0:T(128)} %param.13, s32[]{:T(128)S(6)} %select_n.24, s32[]{:T(128)S(6)} %select_n.25), kind=kLoop, calls=%fused_computation.52 | loop fusion | bytes 520 | tf_op jit(solution)/shard_map/dynamic_slice | solution.py:26
  7.4 0.1 add_select_fusion
  7.5 0.1 select_n.27
  7.5 1.0 %bitcast_convert_fusion = f32[1024,128]{1,0:T(8,128)S(1)} fusion(bf16[32,32,128]{2,1,0:T(8,128)(2,1)} %param.12), kind=kLoop, calls=%fused_computation.36 | loop fusion | flops 131072 | bytes 786432 | tf_op jit(solution)/shard_map/convert_element_type | solution.py:33
  8.5 0.0 copy-start.3
  8.5 0.0 copy-start.5
  8.5 0.2 copy.21
  8.7 0.0 copy-done.2
  8.8 1.0 %fusion.28 = (f32[1024]{0:T(1024)S(1)}, f32[1024,128]{0,1:T(8,128)S(1)}) fusion(f32[1024,128]{0,1:T(8,128)S(1)} %copy.21, bf16[128,128]{1,0:T(8,128)(2,1)S(1)} %copy-done.2, s32[1024]{0:T(1024)S(1)} %select_n.27), kind=kOutput, calls=%fused_computation.53 | convolution fusion | flops 33946624 | bytes 1089536 | tf_op jit(solution)/shard_map/dot_general | solution.py:33
  9.7 0.0 copy-start.1
  9.7 0.1 multiply_reduce_fusion
  9.8 0.0 copy-start.4
  9.8 0.0 copy-done.3
  9.9 0.0 copy-done.5
  9.9 0.2 convolution_bitcast_fusion
  10.1 0.1 reshape.112
  10.2 0.8 reshape.122
  11.0 6.3 %all-to-all-start = ((f32[4,1,4096]{2,1,0:T(1,128)}), f32[4,1,4096]{2,1,0:T(1,128)S(1)}, u32[]{:S(2)}, u32[]{:S(2)}) async-start(f32[4,1,4096]{2,1,0:T(1,128)} %reshape.122), calls=%async_computation | async-start | bytes 131072 | tf_op jit(solution)/shard_map/all_to_all | solution.py:80
  17.3 0.0 all-gather.3.cloned.1.call-start
  17.4 0.7 all-gather.3.cloned.1.call-update
  18.1 0.0 copy-done.1
  18.1 0.1 convert_reduce_fusion
  18.2 0.2 fusion.19
  18.4 0.0 copy-done.4
  18.4 0.1 fusion.21
  18.6 24.0 %all_gather.9 = bf16[4,128,768]{2,1,0:T(8,128)(2,1)S(1)} all-gather(bf16[4,32,768]{2,1,0:T(8,128)(2,1)S(1)} %fusion.21), channel_id=1, replica_groups=mesh['job'=2,'row'=4,'col'=2,'samp'=2] {'row'}, dimensions={1}, use_global_device_ids=true | all-gather | bytes 983040 | tf_op jit(solution)/shard_map/all_gather | solution.py:93
  42.6 0.0 copy-done
  42.6 0.6 fusion.10
  43.3 0.0 all-to-all-done
  43.3 0.5 broadcast.98
  43.8 0.8 %reduce.1 = f32[4,4096]{1,0:T(4,128)S(1)} reduce(f32[4,1,4096]{2,1,0:T(1,128)S(1)} %all-to-all-done, f32[]{:T(128)} %broadcast.98), dimensions={1}, to_apply=%all_to_all.24.reduce_sub_computation | reduce | bytes 131076 | tf_op jit(solution)/shard_map/all_to_all | solution.py:80
  44.7 0.1 reshape.123
  44.8 0.1 copy.22
  44.9 0.2 all_to_all.27
  45.1 5.8 %all_gather.10 = f32[4,128,128]{1,2,0:T(8,128)S(1)} all-gather(f32[4,128,32]{1,2,0:T(8,128)S(1)} %all_to_all.27), channel_id=1, replica_groups=mesh['job'=2,'row'=4,'col'=2,'samp'=2] {'col','samp'}, dimensions={2}, use_global_device_ids=true | all-gather | bytes 327680 | tf_op jit(solution)/shard_map/all_gather | solution.py:81
  50.9 5.3 %while.11 = (s32[]{:T(128)}, bf16[4,128,192]{1,2,0:T(8,128)(2,1)S(1)}, bf16[4,128,192]{1,2,0:T(8,128)(2,1)S(1)}, bf16[4,128,192]{1,2,0:T(8,128)(2,1)S(1)}, bf16[...) while((s32[]{:T(128)}, ...), condition=%wide.region_7.8_spmd.clone, body=%wide.region_4.7_spmd.clone.sunk | while | flops 13263744 | bytes 1643109 | solution.py:97
  50.9 0.6 iota_compare_fusion.4
  51.5 0.2 fusion.49
  51.8 0.1 fusion.50
  51.9 0.2 convolution_convert_fusion.3
  52.2 0.7 iota_compare_fusion.4
  52.9 0.2 fusion.49
  53.1 0.1 fusion.50
  53.3 0.2 convolution_convert_fusion.3
  53.6 0.7 iota_compare_fusion.4
  54.2 0.2 fusion.49
  54.5 0.1 fusion.50
  54.6 0.2 convolution_convert_fusion.3
  54.9 0.7 iota_compare_fusion.4
  55.6 0.2 fusion.49
  55.8 0.1 fusion.50
  55.9 0.2 convolution_convert_fusion.3
  56.2 0.2 copy.23
  56.4 14.7 %all_to_all.33 = bf16[4,128,192]{2,0,1:T(4,128)(2,1)S(1)} all-to-all(bf16[4,128,192]{2,0,1:T(4,128)(2,1)S(1)} %copy.23), channel_id=1, replica_groups=mesh['job'=2,'row'=4,'col'=2,'samp'=2] {'row'}, dimensions={1} | all-to-all | bytes 393216 | tf_op jit(solution)/shard_map/all_to_all | solution.py:98
  71.2 0.2 copy.25
  71.4 0.2 dot_general.26
  71.6 0.0 all-gather.3.cloned.1.call-done
  71.7 2.3 %fusion.12 = bf16[4,32,768]{2,1,0:T(8,128)(2,1)} fusion(bf16[4,32,768]{2,1,0:T(8,128)(2,1)S(1)} %dot_general.26, bf16[1,768,768]{2,1,0:T(8,128)(2,1)} %all-gather.3.cloned.1.call-done, bf16[4,32,768]{2,1,0:T(8,128)(2,1)S(1)} %copy-done.1), kind=kOutput, calls=%fused_computation.22 | convolution fusion | flops 151289856 | bytes 1769472 | tf_op jit(solution)/shard_map/dot_general | solution.py:100
  (21 shorter events, 0.3 us)
Async XLA Ops:
  6.5 36.1 %copy-start = (bf16[1,3,768,192]{2,3,1,0:T(8,128)(2,1)S(1)}, bf16[1,3,768,192]{2,3,1,0:T(8,128)(2,1)}, u32[]{:S(2)}) copy-start(bf16[1,3,768,192]{2,3,1,0:T(8,128)(2,1)} %param.20) | copy-start | bytes 2654212
  6.5 2.2 %copy-start.2 = (bf16[128,128]{1,0:T(8,128)(2,1)S(1)}, bf16[128,128]{1,0:T(8,128)(2,1)}, u32[]{:S(2)}) copy-start(bf16[128,128]{1,0:T(8,128)(2,1)} %param.15) | copy-start | bytes 98308
  8.5 1.3 %copy-start.3 = (bf16[128,16]{0,1:T(8,128)(2,1)S(1)}, bf16[128,16]{0,1:T(8,128)(2,1)}, u32[]{:S(2)}) copy-start(bf16[128,16]{0,1:T(8,128)(2,1)} %param.17) | copy-start | bytes 12292
  8.5 1.3 %copy-start.5 = (f32[128]{0:T(128)S(1)}, f32[128]{0:T(128)}, u32[]{:S(2)}) copy-start(f32[128]{0:T(128)} %param.16) | copy-start | bytes 1540
  9.7 8.4 %copy-start.1 = (bf16[4,32,768]{2,1,0:T(8,128)(2,1)S(1)}, bf16[4,32,768]{2,1,0:T(8,128)(2,1)}, u32[]{:S(2)}) copy-start(bf16[4,32,768]{2,1,0:T(8,128)(2,1)} %param.18) | copy-start | bytes 589828
  9.8 8.6 %copy-start.4 = (f32[1,768]{1,0:T(1,128)S(1)}, f32[1,768]{1,0:T(1,128)}, u32[]{:S(2)}) copy-start(f32[1,768]{1,0:T(1,128)} %param.19) | copy-start | bytes 9220
  11.0 32.3 %all-to-all-start = ((f32[4,1,4096]{2,1,0:T(1,128)}), f32[4,1,4096]{2,1,0:T(1,128)S(1)}, u32[]{:S(2)}, u32[]{:S(2)}) async-start(f32[4,1,4096]{2,1,0:T(1,128)} %reshape.122), calls=%async_computation | async-start | bytes 131072 | tf_op jit(solution)/shard_map/all_to_all | solution.py:80
  17.3 54.3 %all-gather.3.cloned.1.call-start = ((), (), s32[]{:S(2)}) async-start(), calls=%async_computation.2 | async-start | bytes 1474560 | tf_op jit(solution)/shard_map/all_gather | solution.py:102
Sparse Core Ops, SparseCore 0:
  19.7 35.6 all-gather.2
where the time goes:
time: 81.1 us; the launch traced here: 80.8 us
  blocking collectives  44.5 us (55%)
  between operations  13.6 us (17%)
  starting transfers between devices  6.35 us (8%)
  matrix products  6.03 us (7%)
  other arithmetic  5.46 us (7%)
  local copies, waits for them, and re-layouts  3.84 us (5%)
    all_gather x1, blocking collectives, per_device(): lax.all_gather(normed, 'row', axis=1, tiled=True)  24 us
    all_to_all x1, blocking collectives, per_device(): lax.all_to_all(head_out, 'row', split_axis=1, concat_axis=2, tiled=True)  14.7 us
    all_to_all x1, starting transfers between devices, per_device(): lax.all_to_all(bias_tile, 'row', split_axis=0, concat_axis=1, tiled=True)  6.35 us
    all_gather x1, blocking collectives, per_device(): pair_bias = lax.all_gather(head_tile, ('col', 'samp'), axis=2, tiled=True)  5.78 us
    lt x4, other arithmetic, per_device(): keymask = jnp.arange(total_tokens, dtype=jnp.int32) < valid_len[0]  2.61 us
    dot_general x1, matrix products, per_device(): jnp.dot(flattened, lax.all_gather(out_weight[0], 'row', axis=0, tiled=Tru...  2.28 us
  transfers between devices with their start and end apart: 2, of which 0 were waited for; matrix products, arithmetic and copies ran while one was open for 11% of the time, Pallas kernels for 0%

commit v1 on v0

--- a/solution.py
+++ b/solution.py
@@ -6,6 +6,20 @@
 
 HEAD_DIM = 48
 epsilon = 1e-05
+
+
+def on_each_block(array, axis, dim, make, out_dim):
+    ways, here, lap = (lax.axis_size(axis), lax.axis_index(axis), array.shape[dim])
+    earlier, later = ([], [])
+    going_up = going_down = array
+    for far in range(ways // 2 + 1):
+        earlier.append(make(going_up, (here - far) % ways * lap))
+        if 0 < far < ways - ways // 2:
+            later.append(make(going_down, (here + far) % ways * lap))
+        going_up = lax.ppermute(going_up, axis, [(d, (d + 1) % ways) for d in range(ways)])
+        going_down = lax.ppermute(going_down, axis, [(d, (d - 1) % ways) for d in range(ways)])
+    line = jnp.concatenate([*earlier[::-1], *later], axis=out_dim)
+    return jnp.roll(line, (here - ways // 2) * earlier[0].shape[out_dim], axis=out_dim)
 
 
 def normalize(values, gain_vector):
@@ -88,11 +102,14 @@
     current = tokens
     normed = normalize(current.astype(jnp.float32), token_gain[0]).astype(jnp.bfloat16)
     layer_weight = qkv_weight[0]
-    projected = jnp.einsum(
-        "snc,pcw->psnw",
-        lax.all_gather(normed, "row", axis=1, tiled=True),
-        layer_weight,
-        preferred_element_type=jnp.float32,
+    projected = on_each_block(
+        normed,
+        "row",
+        1,
+        lambda part, start: jnp.einsum(
+            "snc,pcw->psnw", part, layer_weight, preferred_element_type=jnp.float32
+        ),
+        2,
     ).astype(jnp.bfloat16)
     head_out = lax.map(one_sample, (projected[0], projected[1], projected[2]))
     attended = lax.all_to_all(head_out, "row", split_axis=1, concat_axis=2, tiled=True)

time: 81.1 us -> 71.8 us (0.89)
  blocking collectives: 44.5 us -> 21.3 us
  starting transfers between devices: 6.35 us -> 10.8 us
  waiting for transfers between devices: 0.73 us -> 4.63 us
  other arithmetic: 5.46 us -> 9.07 us
  matrix products: 6.03 us -> 7.14 us
    all_gather x1 -> x0, blocking collectives: 24 us -> none  [per_device(): lax.all_gather(normed, 'row', axis=1, tiled=True)]
    ppermute x0 -> x3, starting transfers between devices: none -> 6.99 us  [the longest x2 5.13 us: on_each_block(): lax.ppermute(going_up, axis, [(d, (d + 1) % ways) for d in range(ways)])]
    all_to_all x1, waiting for transfers between devices: 0.01 us -> 4.58 us  [per_device(): lax.all_to_all(bias_tile, 'row', split_axis=0, concat_axis=1, tiled=True)]
    all_to_all x1, starting transfers between devices: 6.35 us -> 3.86 us  [per_device(): lax.all_to_all(bias_tile, 'row', split_axis=0, concat_axis=1, tiled=True)]
    dot_general x1 -> x4, matrix products: 0.65 us -> 1.76 us  [per_device(): jnp.einsum('snc,pcw->psnw', part, layer_weight, preferred_element_type=jn...]
    reduce_sum x1, other arithmetic: 0.11 us -> 1.12 us  [normalize(): average = jnp.mean(values, axis=-1, keepdims=True)]
    convert_element_type x1, other arithmetic: 0.15 us -> 1.09 us  [per_device(): normalize(current.astype(jnp.float32), token_gain[0]).astype(jnp.bfloat16)]
    reduce_sum x2, other arithmetic: 0.26 us -> 1.19 us  [normalize(): variance = jnp.mean(centered * centered, axis=-1, keepdims=True)]
  transfers between devices with their start and end apart: 2 -> 5, of which waited for: 0 -> 1; matrix products, arithmetic and copies ran while one was open for 11% -> 20% of each run, Pallas kernels for 0% -> 0%
where the time goes in v1:
time: 71.8 us; the launch traced here: 71.4 us
  blocking collectives  21.3 us (30%)
  between operations  13.7 us (19%)
  starting transfers between devices  10.8 us (15%)
  other arithmetic  9.07 us (13%)
  matrix products  7.14 us (10%)
  waiting for transfers between devices  4.63 us (6%)
  local copies, waits for them, and re-layouts  4.44 us (6%)
    all_to_all x1, blocking collectives, per_device(): lax.all_to_all(head_out, 'row', split_axis=1, concat_axis=2, tiled=True)  15.5 us
    all_gather x1, blocking collectives, per_device(): pair_bias = lax.all_gather(head_tile, ('col', 'samp'), axis=2, tiled=True)  5.78 us
    ppermute x2, starting transfers between devices, on_each_block(): lax.ppermute(going_up, axis, [(d, (d + 1) % ways) for d in range(ways)])  5.13 us
    all_to_all x1, waiting for transfers between devices, per_device(): lax.all_to_all(bias_tile, 'row', split_axis=0, concat_axis=1, tiled=True)  4.58 us
    all_to_all x1, starting transfers between devices, per_device(): lax.all_to_all(bias_tile, 'row', split_axis=0, concat_axis=1, tiled=True)  3.86 us
    lt x4, other arithmetic, per_device(): keymask = jnp.arange(total_tokens, dtype=jnp.int32) < valid_len[0]  2.61 us
    dot_general x1, matrix products, per_device(): jnp.dot(flattened, lax.all_gather(out_weight[0], 'row', axis=0, tiled=Tru...  2.28 us
    ppermute x1, starting transfers between devices, on_each_block(): lax.ppermute(going_down, axis, [(d, (d - 1) % ways) for d in range(ways)])  1.86 us
  transfers between devices with their start and end apart: 5, of which 1 were waited for; matrix products, arithmetic and copies ran while one was open for 20% of the time, Pallas kernels for 0%

profile of v1, /device:TPU:0, one launch (start us, length us, event | category | flops | bytes accessed | tf_op | source)
XLA Modules:
  0.0 71.4 jit_solution(16313440501116665942)
XLA Ops:
  6.5 0.0 copy-start
  6.5 1.1 %convert_reduce_fusion = f32[4,32]{1,0:T(4,128)S(1)} fusion(bf16[4,32,768]{2,1,0:T(8,128)(2,1)} %param.18), kind=kLoop, calls=%fused_computation.32 | loop fusion | flops 196480 | bytes 197120 | tf_op jit(solution)/shard_map/reduce_sum | solution.py:26
  7.7 1.1 %fusion.20 = f32[4,32]{1,0:T(4,128)S(1)} fusion(bf16[4,32,768]{2,1,0:T(8,128)(2,1)} %param.18, f32[4,32]{1,0:T(4,128)S(1)} %broadcast_multiply_fusion.1), kind=kLoop, calls=%fused_computation.38 | loop fusion | flops 393088 | bytes 197632 | tf_op jit(solution)/shard_map/reduce_sum | solution.py:28
  8.8 0.7 reduce
  9.5 1.1 %fusion.22 = bf16[4,32,768]{2,1,0:T(8,128)(2,1)S(1)} fusion(bf16[4,32,768]{2,1,0:T(8,128)(2,1)} %param.18, f32[768]{0:T(1024)S(1)} %reduce, f32[4,32]{1,0:T(4,128)S(1)} %add_rsqrt_fusion.1, f32[4,32]{1,0:T(4,128)S(1)} %broadcast_multiply_fusion.1), kind=kLoop, calls=%fused_computation.40 | loop fusion | flops 491520 | bytes 397312 | tf_op jit(solution)/shard_map/convert_element_type | solution.py:103
  10.6 3.1 %collective-permute-start = (bf16[4,32,768]{2,1,0:T(8,128)(2,1)S(1)}, bf16[4,32,768]{2,1,0:T(8,128)(2,1)S(1)}, u32[]{:S(2)}, u32[]{:S(2)}) collective-permute-start(bf16[4,32,768]{2,1,0:T(8,128)(2,1)S(1)} %fusion.22), channel_id=1, source_target_pairs={{0,4},{4,8},{8,12},{12,0},{1,5},{5,9},{9,13},{13,1},{2,6},{6,10},{... | collective-permute-start | bytes 589832 | tf_op jit(solution)/shard_map/ppermute | solution.py:19
  13.7 0.8 %fusion.32 = (s32[32]{0:T(128)S(1)}, s32[32]{0:T(128)S(1)}) fusion(s32[128]{0:T(128)} %param.13, s32[]{:T(128)S(6)} %select_n.39, s32[]{:T(128)S(6)} %select_n.40), kind=kLoop, calls=%fused_computation.69 | loop fusion | bytes 520 | tf_op jit(solution)/shard_map/dynamic_slice | solution.py:40
  14.5 0.1 add_select_fusion
  14.6 0.1 select_n.42
  14.7 1.0 %bitcast_convert_fusion = f32[1024,128]{1,0:T(8,128)S(1)} fusion(bf16[32,32,128]{2,1,0:T(8,128)(2,1)} %param.12), kind=kLoop, calls=%fused_computation.44 | loop fusion | flops 131072 | bytes 786432 | tf_op jit(solution)/shard_map/convert_element_type | solution.py:47
  15.7 0.2 copy.27
  15.9 1.0 %fusion.33 = (f32[1024]{0:T(1024)S(1)}, f32[1024,128]{0,1:T(8,128)S(1)}) fusion(f32[1024,128]{0,1:T(8,128)S(1)} %copy.27, bf16[128,128]{1,0:T(8,128)(2,1)S(1)} %copy-done.2, s32[1024]{0:T(1024)S(1)} %select_n.42), kind=kOutput, calls=%fused_computation.70 | convolution fusion | flops 33946624 | bytes 1089536 | tf_op jit(solution)/shard_map/dot_general | solution.py:47
  16.9 0.1 multiply_reduce_fusion
  17.0 0.2 convolution_bitcast_fusion.4
  17.2 0.1 reshape.112
  17.3 0.8 %reshape.125 = f32[4,1,4096]{2,1,0:T(1,128)} reshape(f32[16,32,32]{2,1,0:T(8,128)S(1)} %reshape.112) | data formatting | bytes 131072
  18.1 3.9 %all-to-all-start = ((f32[4,1,4096]{2,1,0:T(1,128)}), f32[4,1,4096]{2,1,0:T(1,128)S(1)}, u32[]{:S(2)}, u32[]{:S(2)}) async-start(f32[4,1,4096]{2,1,0:T(1,128)} %reshape.125), calls=%async_computation | async-start | bytes 131072 | tf_op jit(solution)/shard_map/all_to_all | solution.py:94
  22.0 0.0 collective-permute-done
  22.0 2.0 %collective-permute-start.1 = (bf16[4,32,768]{2,1,0:T(8,128)(2,1)S(1)}, bf16[4,32,768]{2,1,0:T(8,128)(2,1)S(1)}, u32[]{:S(2)}, u32[]{:S(2)}) collective-permute-start(bf16[4,32,768]{2,1,0:T(8,128)(2,1)S(1)} %collective-permute-done), channel_id=1, source_target_pairs={{0,4},{4,8},{8,12},{12,0},{1,5},{5,9},{9,13},{13,1},{2,6},{6,10},{... | collective-permute-start | bytes 589832 | tf_op jit(solution)/shard_map/ppermute | solution.py:19
  24.0 1.9 %collective-permute-start.2 = (bf16[4,32,768]{2,1,0:T(8,128)(2,1)S(1)}, bf16[4,32,768]{2,1,0:T(8,128)(2,1)S(1)}, u32[]{:S(2)}, u32[]{:S(2)}) collective-permute-start(bf16[4,32,768]{2,1,0:T(8,128)(2,1)S(1)} %fusion.22), channel_id=1, source_target_pairs={{0,12},{4,0},{8,4},{12,8},{1,13},{5,1},{9,5},{13,9},{2,14},{6,2},{... | collective-permute-start | bytes 589832 | tf_op jit(solution)/shard_map/ppermute | solution.py:20
  25.9 0.0 all-gather.3.cloned.1.call-update
  25.9 4.6 %all-to-all-done = f32[4,1,4096]{2,1,0:T(1,128)S(1)} async-done(((f32[4,1,4096]{2,1,0:T(1,128)}), f32[4,1,4096]{2,1,0:T(1,128)S(1)}, u32[]{:S(2)}, u32[]{:S(2)}) %all-to-all-start) | async-done | bytes 65568 | tf_op jit(solution)/shard_map/all_to_all | solution.py:94
  30.5 0.5 broadcast.99
  31.0 0.8 %reduce.1 = f32[4,4096]{1,0:T(4,128)S(1)} reduce(f32[4,1,4096]{2,1,0:T(1,128)S(1)} %all-to-all-done, f32[]{:T(128)} %broadcast.99), dimensions={1}, to_apply=%all_to_all.24.reduce_sub_computation | reduce | bytes 131076 | tf_op jit(solution)/shard_map/all_to_all | solution.py:94
  31.9 0.1 reshape.126
  32.0 0.1 copy.28
  32.1 0.2 all_to_all.27
  32.3 5.8 %all_gather.6 = f32[4,128,128]{1,2,0:T(8,128)S(1)} all-gather(f32[4,128,32]{1,2,0:T(8,128)S(1)} %all_to_all.27), channel_id=1, replica_groups=mesh['job'=2,'row'=4,'col'=2,'samp'=2] {'col','samp'}, dimensions={2}, use_global_device_ids=true | all-gather | bytes 327680 | tf_op jit(solution)/shard_map/all_gather | solution.py:95
  38.1 0.0 collective-permute-done.1
  38.1 0.0 copy-done
  38.1 0.4 constant_dynamic-update-slice_fusion.8
  38.5 0.4 constant_dynamic-update-slice_fusion.7
  39.0 0.4 constant_dynamic-update-slice_fusion.6
  39.4 0.0 collective-permute-done.2
  39.4 0.4 constant_dynamic-update-slice_fusion.5
  40.0 0.1 dynamic-slice_convert_fusion
  40.1 0.1 slice_bitcast_fusion
  40.1 0.2 copy.29
  40.3 0.2 copy.30
  40.5 0.2 copy.31
  40.6 5.3 %while.11 = (s32[]{:T(128)}, bf16[4,128,192]{1,2,0:T(8,128)(2,1)S(1)}, bf16[4,128,192]{1,2,0:T(8,128)(2,1)S(1)}, bf16[4,128,192]{1,2,0:T(8,128)(2,1)S(1)}, bf16[...) while((s32[]{:T(128)}, ...), condition=%wide.region_7.8_spmd.clone, body=%wide.region_4.7_spmd.clone.sunk | while | flops 13263744 | bytes 1643109 | solution.py:114
  40.7 0.7 iota_compare_fusion.4
  41.3 0.2 fusion.54
  41.6 0.1 fusion.55
  41.7 0.2 convolution_convert_fusion.2
  42.0 0.7 iota_compare_fusion.4
  42.7 0.2 fusion.54
  42.9 0.1 fusion.55
  43.0 0.2 convolution_convert_fusion.2
  43.3 0.7 iota_compare_fusion.4
  44.0 0.2 fusion.54
  44.2 0.1 fusion.55
  44.4 0.2 convolution_convert_fusion.2
  44.7 0.7 iota_compare_fusion.4
  45.3 0.2 fusion.54
  45.6 0.1 fusion.55
  45.7 0.2 convolution_convert_fusion.2
  46.0 0.0 copy-start.1
  46.0 0.2 copy.32
  46.2 15.5 %all_to_all.33 = bf16[4,128,192]{2,0,1:T(4,128)(2,1)S(1)} all-to-all(bf16[4,128,192]{2,0,1:T(4,128)(2,1)S(1)} %copy.32), channel_id=1, replica_groups=mesh['job'=2,'row'=4,'col'=2,'samp'=2] {'row'}, dimensions={1} | all-to-all | bytes 393216 | tf_op jit(solution)/shard_map/all_to_all | solution.py:115
  61.8 0.2 copy.34
  62.0 0.2 dot_general.38
  62.2 0.0 all-gather.3.cloned.1.call-done
  62.2 2.3 %fusion.11 = bf16[4,32,768]{2,1,0:T(8,128)(2,1)} fusion(bf16[4,32,768]{2,1,0:T(8,128)(2,1)S(1)} %dot_general.38, bf16[1,768,768]{2,1,0:T(8,128)(2,1)} %all-gather.3.cloned.1.call-done, bf16[4,32,768]{2,1,0:T(8,128)(2,1)S(1)} %copy-done.1), kind=kOutput, calls=%fused_computation.25 | convolution fusion | flops 151289856 | bytes 1769472 | tf_op jit(solution)/shard_map/dot_general | solution.py:117
  (31 shorter events, 0.3 us)
Async XLA Ops:
  6.5 31.6 %copy-start = (bf16[1,3,768,192]{2,3,1,0:T(8,128)(2,1)S(1)}, bf16[1,3,768,192]{2,3,1,0:T(8,128)(2,1)}, u32[]{:S(2)}) copy-start(bf16[1,3,768,192]{2,3,1,0:T(8,128)(2,1)} %param.20) | copy-start | bytes 2654212
  6.5 9.4 %copy-start.2 = (bf16[128,128]{1,0:T(8,128)(2,1)S(1)}, bf16[128,128]{1,0:T(8,128)(2,1)}, u32[]{:S(2)}) copy-start(bf16[128,128]{1,0:T(8,128)(2,1)} %param.15) | copy-start | bytes 98308
  10.6 11.4 %collective-permute-start = (bf16[4,32,768]{2,1,0:T(8,128)(2,1)S(1)}, bf16[4,32,768]{2,1,0:T(8,128)(2,1)S(1)}, u32[]{:S(2)}, u32[]{:S(2)}) collective-permute-start(bf16[4,32,768]{2,1,0:T(8,128)(2,1)S(1)} %fusion.22), channel_id=1, source_target_pairs={{0,4},{4,8},{8,12},{12,0},{1,5},{5,9},{9,13},{13,1},{2,6},{6,10},{... | collective-permute-start | bytes 589832 | tf_op jit(solution)/shard_map/ppermute | solution.py:19
  14.7 2.3 %copy-start.3 = (bf16[128,16]{0,1:T(8,128)(2,1)S(1)}, bf16[128,16]{0,1:T(8,128)(2,1)}, u32[]{:S(2)}) copy-start(bf16[128,16]{0,1:T(8,128)(2,1)} %param.17) | copy-start | bytes 12292
  14.7 2.3 %copy-start.4 = (f32[128]{0:T(128)S(1)}, f32[128]{0:T(128)}, u32[]{:S(2)}) copy-start(f32[128]{0:T(128)} %param.16) | copy-start | bytes 1540
  18.1 12.4 %all-to-all-start = ((f32[4,1,4096]{2,1,0:T(1,128)}), f32[4,1,4096]{2,1,0:T(1,128)S(1)}, u32[]{:S(2)}, u32[]{:S(2)}) async-start(f32[4,1,4096]{2,1,0:T(1,128)} %reshape.125), calls=%async_computation | async-start | bytes 131072 | tf_op jit(solution)/shard_map/all_to_all | solution.py:94
  22.0 40.2 %all-gather.3.cloned.1.call-start = ((), (), s32[]{:S(2)}) async-start(), calls=%async_computation.2 | async-start | bytes 1474560 | tf_op jit(solution)/shard_map/all_gather | solution.py:119
  22.0 16.1 %collective-permute-start.1 = (bf16[4,32,768]{2,1,0:T(8,128)(2,1)S(1)}, bf16[4,32,768]{2,1,0:T(8,128)(2,1)S(1)}, u32[]{:S(2)}, u32[]{:S(2)}) collective-permute-start(bf16[4,32,768]{2,1,0:T(8,128)(2,1)S(1)} %collective-permute-done), channel_id=1, source_target_pairs={{0,4},{4,8},{8,12},{12,0},{1,5},{5,9},{9,13},{13,1},{2,6},{6,10},{... | collective-permute-start | bytes 589832 | tf_op jit(solution)/shard_map/ppermute | solution.py:19
  24.0 15.4 %collective-permute-start.2 = (bf16[4,32,768]{2,1,0:T(8,128)(2,1)S(1)}, bf16[4,32,768]{2,1,0:T(8,128)(2,1)S(1)}, u32[]{:S(2)}, u32[]{:S(2)}) collective-permute-start(bf16[4,32,768]{2,1,0:T(8,128)(2,1)S(1)} %fusion.22), channel_id=1, source_target_pairs={{0,12},{4,0},{8,4},{12,8},{1,13},{5,1},{9,5},{13,9},{2,14},{6,2},{... | collective-permute-start | bytes 589832 | tf_op jit(solution)/shard_map/ppermute | solution.py:20
  46.0 16.2 %copy-start.1 = (bf16[4,32,768]{2,1,0:T(8,128)(2,1)S(1)}, bf16[4,32,768]{2,1,0:T(8,128)(2,1)}, u32[]{:S(2)}) copy-start(bf16[4,32,768]{2,1,0:T(8,128)(2,1)} %param.18) | copy-start | bytes 589828
Sparse Core Ops, SparseCore 0:
  26.0 34.2 all-gather.2
